TPU v7x, 32 devices: a whole 2x2x4 slice. The times are simulated.
32 devices in a mesh: gx: 4 (over y, core), gy: 8 (over z, x).
Axes of the slice: x: 2, y: 2, z: 4, core: 2. Of those that a mesh axis runs over, the one named last changes fastest.
Arguments:
- particle_cell: int32 [4, 8, 65536], P('gx', 'gy'), may hold values from -1 to 16383, as said below
- particle_mass: float32 [4, 8, 65536], P('gx', 'gy'), may hold values from 0.5 to 2
Outputs:
- potential: float32 [64, 64, 128], P('gx', 'gy')
- residual: float32 [64, 64, 128], P('gx', 'gy')
- residual_norms: float32 [2], replicated
Inputs may be any that keep to these rules, and one draw needn't show every extreme that they name: `particle_cell`: -1 marks an empty slot; any other value v names the cell (v // 1024, v // 128 % 8, v % 128) of the block of 16 x 8 x 128 cells that belongs to the slot's tile.
All inputs are finite; a program needn't handle non-finite values.
Results may differ from a plain program's by a relative error of at most 0.0003.
Values sent between devices are 32-bit elements; how exact they have to be, the bound alone decides.
A program may use at most 64 MiB of HBM per device.

v0:
```python
import jax
import jax.numpy as jnp
from jax import lax
from jax.sharding import PartitionSpec as P

CX = 16
CY = 8
NZ = 128
LEVELS = 4
CYCLES = 2
COARSE_SWEEPS = 2


coupling = 0.03125
norm_eps = 1e-06


def with_halo(cells, sides, width):
    for axis, dim in sides:
        count = lax.axis_size(axis)
        head = lax.slice_in_dim(cells, 0, width, axis=dim)
        tail = lax.slice_in_dim(cells, cells.shape[dim] - width, cells.shape[dim], axis=dim)
        cells = jnp.concatenate(
            [
                lax.ppermute(tail, axis, [(i, (i + 1) % count) for i in range(count)]),
                cells,
                lax.ppermute(head, axis, [((i + 1) % count, i) for i in range(count)]),
            ],
            axis=dim,
        )
    return cells


def parity_mask(shape, start_x, start_y):
    index_x = jnp.arange(shape[0], dtype=jnp.int32)[:, None, None] + start_x
    index_y = jnp.arange(shape[1], dtype=jnp.int32)[None, :, None] + start_y
    index_z = jnp.arange(shape[2], dtype=jnp.int32)[None, None, :]
    return (index_x + index_y + index_z) % 2 == 0


def restrict(values):
    rows_x, rows_y, rows_z = values.shape
    return values.reshape(rows_x // 2, 2, rows_y // 2, 2, rows_z // 2, 2).mean(axis=(1, 3, 5))


def prolong(values):
    rows_x, rows_y, rows_z = values.shape
    spread = jnp.broadcast_to(values[:, None, :, None, :, None], (rows_x, 2, rows_y, 2, rows_z, 2))
    return spread.reshape(2 * rows_x, 2 * rows_y, 2 * rows_z)


def narrow_pad(values):
    return with_halo(values, (("gx", 0), ("gy", 1)), 1)


def edge_sum(padded):
    centre = padded[1:-1, 1:-1]
    beside = padded[:-2, 1:-1] + padded[2:, 1:-1]
    beside = beside + padded[1:-1, :-2] + padded[1:-1, 2:]
    return (centre, beside + jnp.roll(centre, 1, 2) + jnp.roll(centre, -1, 2))


def relax_colour(padded, source, chosen, spacing_squared):
    centre, beside = edge_sum(padded)
    updated = (beside + spacing_squared * source) / 6.0
    return jnp.where(chosen, updated, centre)


def local_residual(estimate, source, spacing_squared):
    centre, beside = edge_sum(narrow_pad(estimate))
    return source - (6.0 * centre - beside) / spacing_squared


def per_device(particle_cell, particle_mass):
    block_cells = CX * CY * NZ
    tiles_x = lax.axis_size("gx")
    tiles_y = lax.axis_size("gy")
    tile_x = lax.axis_index("gx")
    tile_y = lax.axis_index("gy")
    grid_cells = block_cells * tiles_x * tiles_y
    slot_ids = particle_cell.reshape(-1)
    masses = particle_mass.reshape(-1)
    occupied = slot_ids >= 0
    target = jnp.where(occupied, slot_ids, block_cells)
    density = jnp.zeros((block_cells + 1,), jnp.float32).at[target].add(masses)[:block_cells]
    density = density.reshape(CX, CY, NZ)
    total_mass = lax.psum(jnp.sum(jnp.where(occupied, masses, 0.0)), ("gx", "gy"))
    mean_mass = total_mass / grid_cells
    source = coupling * (1.0 - density / mean_mass)

    def deep_pad(values):
        return with_halo(values, (("gx", 0), ("gy", 1)), 2)

    def smooth_level(estimate, level_source, spacing_squared, wide_source):
        rows_x, rows_y, rows_z = estimate.shape
        start_x = tile_x * rows_x
        start_y = tile_y * rows_y
        red_cells = parity_mask(estimate.shape, start_x, start_y)
        black_cells = jnp.logical_not(red_cells)
        if wide_source is None:
            estimate = relax_colour(narrow_pad(estimate), level_source, red_cells, spacing_squared)
            return relax_colour(narrow_pad(estimate), level_source, black_cells, spacing_squared)
        wide_red = parity_mask((rows_x + 2, rows_y + 2, rows_z), start_x - 1, start_y - 1)
        grown_field = relax_colour(deep_pad(estimate), wide_source, wide_red, spacing_squared)
        return relax_colour(grown_field, level_source, black_cells, spacing_squared)

    def multigrid_cycle(grid_level, estimate, level_source):
        spacing_squared = float(4**grid_level)
        wide_source = None
        if deep_pad is not None and min(estimate.shape[0], estimate.shape[1]) >= 2:
            wide_source = deep_pad(level_source)[1:-1, 1:-1]
        if grid_level == LEVELS - 1:
            for repeat in range(COARSE_SWEEPS):
                estimate = smooth_level(estimate, level_source, spacing_squared, wide_source)
            return estimate
        estimate = smooth_level(estimate, level_source, spacing_squared, wide_source)
        coarse_source = restrict(local_residual(estimate, level_source, spacing_squared))
        correction = multigrid_cycle(grid_level + 1, jnp.zeros_like(coarse_source), coarse_source)
        estimate = estimate + prolong(correction)
        return smooth_level(estimate, level_source, spacing_squared, wide_source)

    potential = jnp.zeros((CX, CY, NZ), jnp.float32)
    residual = source
    square_sums = []
    for cycle_index in range(CYCLES):
        potential = multigrid_cycle(0, potential, source)
        residual = local_residual(potential, source, 1.0) / coupling
        square_sum = jnp.sum(residual * residual)
        square_sums.append(lax.psum(square_sum, ("gx", "gy")))
    totals = jnp.stack(square_sums)
    residual_norms = jnp.sqrt(totals / grid_cells + norm_eps)
    return (potential, residual, residual_norms)


def solution(mesh):
    in_specs = (P("gx", "gy", None), P("gx", "gy", None))
    out_specs = (P("gx", "gy", None), P("gx", "gy", None), P())
    return jax.shard_map(
        per_device, mesh=mesh, in_specs=in_specs, out_specs=out_specs, check_vma=False
    )
```

profile of v0, /device:TPU:0, one launch (start us, length us, event | category | flops | bytes accessed | tf_op | source)
XLA Modules:
  0.0 758.7 jit_solution(11418557785699691215)
XLA Ops:
  10.3 360.0 %scatter_custom_fusion = f32[16385]{0:T(1024)S(1)} fusion(s32[65536]{0:T(1024)S(1)} %bitcast.81, f32[65536]{0:T(1024)} %bitcast.80, f32[]{:T(128)} %constant.242.clone.1), kind=kCustom, calls=%fused_computation.247 | custom fusion | flops 65536 | bytes 66052 | tf_op jit(solution)/shard_map/scatter-add | solution.py:85
  370.2 37.1 %psum.21 = f32[]{:T(128)} all-reduce(f32[]{:T(128)} %select_reduce_fusion), channel_id=1, replica_groups=mesh['gx'=4,'gy'=8] {'gx','gy'}, use_global_device_ids=true, to_apply=%region_2.3 | all-reduce | flops 1 | bytes 8 | tf_op jit(solution)/shard_map/psum | solution.py:87
  450.8 5.6 reshape.455
  472.1 4.8 collective-permute-start.27
  482.5 4.8 collective-permute-start.31
  492.4 4.8 collective-permute-start.39
  502.4 4.8 collective-permute-start.43
  512.0 4.8 collective-permute-start.47
  521.7 4.8 collective-permute-start.51
  531.5 4.8 collective-permute-start.55
  542.0 4.8 collective-permute-start.59
  558.9 4.8 collective-permute-start.63
  569.5 4.8 collective-permute-start.67
  580.1 4.8 collective-permute-start.71
  586.6 5.6 reshape.459
  598.0 4.8 collective-permute-start.75
  608.0 4.8 collective-permute-start.79
  618.3 4.8 collective-permute-start.83
  628.2 4.8 collective-permute-start.87
  638.2 4.8 collective-permute-start.91
  647.9 4.8 collective-permute-start.95
  667.3 4.8 collective-permute-start.103
  677.9 4.8 collective-permute-start.107
  716.5 40.4 %all-reduce.3 = (f32[1]{0:T(128)}, f32[1]{0:T(128)}) all-reduce(f32[1]{0:T(128)} %bitcast.11, f32[1]{0:T(128)} %bitcast.10), channel_id=1, replica_groups=mesh['gx'=4,'gy'=8] {'gx','gy'}, use_global_device_ids=true, to_apply=%region_14.15 | all-reduce | flops 2 | bytes 16 | tf_op jit(solution)/shard_map/psum | solution.py:129
  (485 shorter events, 215.8 us)
Async XLA Ops:
  0.6 423.3 %collective-permute-start = (f32[2,8,128]{2,1,0:T(8,128)S(1)}, f32[2,8,128]{2,1,0:T(8,128)S(1)}, u32[]{:S(2)}, u32[]{:S(2)}) collective-permute-start(f32[2,8,128]{2,1,0:T(8,128)S(1)} %broadcast.560), channel_id=1, source_target_pairs={{0,8},{8,16},{16,24},{24,0},{1,9},{9,17},{17,25},{25,1},{2,10},{10... | collective-permute-start | bytes 24584 | tf_op jit(solution)/shard_map/ppermute | solution.py:25
  1.2 427.6 %collective-permute-start.1 = (f32[2,8,128]{2,1,0:T(8,128)S(1)}, f32[2,8,128]{2,1,0:T(8,128)S(1)}, u32[]{:S(2)}, u32[]{:S(2)}) collective-permute-start(f32[2,8,128]{2,1,0:T(8,128)S(1)} %broadcast.560), channel_id=1, source_target_pairs={{8,0},{16,8},{24,16},{0,24},{9,1},{17,9},{25,17},{1,25},{10,2},{18... | collective-permute-start | bytes 24584 | tf_op jit(solution)/shard_map/ppermute | solution.py:27
  3.2 405.4 %collective-permute-start.32 = (f32[1,1,16]{2,0,1:T(1,128)S(1)}, f32[1,1,16]{2,0,1:T(1,128)S(1)}, u32[]{:S(2)}, u32[]{:S(2)}) collective-permute-start(f32[1,1,16]{2,0,1:T(1,128)S(1)} %broadcast.587), channel_id=1, source_target_pairs={{0,8},{8,16},{16,24},{24,0},{1,9},{9,17},{17,25},{25,1},{2,10},{10... | collective-permute-start | bytes 200 | tf_op jit(solution)/shard_map/ppermute | solution.py:25
  3.8 404.9 %collective-permute-start.33 = (f32[1,1,16]{2,0,1:T(1,128)S(1)}, f32[1,1,16]{2,0,1:T(1,128)S(1)}, u32[]{:S(2)}, u32[]{:S(2)}) collective-permute-start(f32[1,1,16]{2,0,1:T(1,128)S(1)} %broadcast.587), channel_id=1, source_target_pairs={{8,0},{16,8},{24,16},{0,24},{9,1},{17,9},{25,17},{1,25},{10,2},{18... | collective-permute-start | bytes 200 | tf_op jit(solution)/shard_map/ppermute | solution.py:27
  4.9 404.3 %collective-permute-start.20 = (f32[2,2,32]{2,0,1:T(2,128)S(1)}, f32[2,2,32]{2,0,1:T(2,128)S(1)}, u32[]{:S(2)}, u32[]{:S(2)}) collective-permute-start(f32[2,2,32]{2,0,1:T(2,128)S(1)} %broadcast.578), channel_id=1, source_target_pairs={{0,8},{8,16},{16,24},{24,0},{1,9},{9,17},{17,25},{25,1},{2,10},{10... | collective-permute-start | bytes 1544 | tf_op jit(solution)/shard_map/ppermute | solution.py:25
  411.4 9.2 %collective-permute-start.4 = (f32[2,8,128]{2,1,0:T(8,128)S(1)}, f32[2,8,128]{2,1,0:T(8,128)S(1)}, u32[]{:S(2)}, u32[]{:S(2)}) collective-permute-start(f32[2,8,128]{2,1,0:T(8,128)S(1)} %get-tuple-element.93), channel_id=1, source_target_pairs={{0,8},{8,16},{16,24},{24,0},{1,9},{9,17},{17,25},{25,1},{2,10},{10... | collective-permute-start | bytes 24584 | tf_op jit(solution)/shard_map/ppermute | solution.py:25
  419.1 79.9 %collective-permute-start.34 = (f32[4,1,16]{2,0,1:T(4,128)S(1)}, f32[4,1,16]{2,0,1:T(4,128)S(1)}, u32[]{:S(2)}, u32[]{:S(2)}) collective-permute-start(f32[4,1,16]{2,0,1:T(4,128)S(1)} %pad_maximum_fusion.199), channel_id=1, source_target_pairs={{0,1},{1,2},{2,3},{3,4},{4,5},{5,6},{6,7},{7,0},{8,9},{9,10},{10,1... | collective-permute-start | bytes 776 | tf_op jit(solution)/shard_map/ppermute | solution.py:25
  420.6 78.4 %collective-permute-start.35 = (f32[4,1,16]{2,0,1:T(4,128)S(1)}, f32[4,1,16]{2,0,1:T(4,128)S(1)}, u32[]{:S(2)}, u32[]{:S(2)}) collective-permute-start(f32[4,1,16]{2,0,1:T(4,128)S(1)} %pad_maximum_fusion.199), channel_id=1, source_target_pairs={{1,0},{2,1},{3,2},{4,3},{5,4},{6,5},{7,6},{0,7},{9,8},{10,9},{11,1... | collective-permute-start | bytes 776 | tf_op jit(solution)/shard_map/ppermute | solution.py:27
  428.7 8.9 %collective-permute-start.6 = (f32[20,2,128]{2,1,0:T(2,128)S(1)}, f32[20,2,128]{2,1,0:T(2,128)S(1)}, u32[]{:S(2)}, u32[]{:S(2)}) collective-permute-start(f32[20,2,128]{2,1,0:T(2,128)S(1)} %get-tuple-element.51), channel_id=1, source_target_pairs={{0,1},{1,2},{2,3},{3,4},{4,5},{5,6},{6,7},{7,0},{8,9},{9,10},{10,1... | collective-permute-start | bytes 61448 | tf_op jit(solution)/shard_map/ppermute | solution.py:25
  430.3 7.0 collective-permute-start.3
  542.0 6.5 collective-permute-start.58
  558.8 6.6 collective-permute-start.62
  558.9 6.5 collective-permute-start.63
  569.4 6.6 collective-permute-start.66
  569.5 6.5 collective-permute-start.67
  597.9 6.5 collective-permute-start.74
  677.8 6.7 collective-permute-start.106
  677.9 6.6 collective-permute-start.107
  682.7 10.7 %collective-permute-start.116 = (f32[1,8,128]{2,1,0:T(8,128)S(1)}, f32[1,8,128]{2,1,0:T(8,128)S(1)}, u32[]{:S(2)}, u32[]{:S(2)}) collective-permute-start(f32[1,8,128]{2,1,0:T(8,128)S(1)} %get-tuple-element.63), channel_id=1, source_target_pairs={{0,8},{8,16},{16,24},{24,0},{1,9},{9,17},{17,25},{25,1},{2,10},{10... | collective-permute-start | bytes 12296 | tf_op jit(solution)/shard_map/ppermute | solution.py:25
  684.0 9.4 %collective-permute-start.117 = (f32[1,8,128]{2,1,0:T(8,128)S(1)}, f32[1,8,128]{2,1,0:T(8,128)S(1)}, u32[]{:S(2)}, u32[]{:S(2)}) collective-permute-start(f32[1,8,128]{2,1,0:T(8,128)S(1)} %get-tuple-element.64), channel_id=1, source_target_pairs={{8,0},{16,8},{24,16},{0,24},{9,1},{17,9},{25,17},{1,25},{10,2},{18... | collective-permute-start | bytes 12296 | tf_op jit(solution)/shard_map/ppermute | solution.py:27
  691.6 6.6 collective-permute-start.108
  693.5 9.6 %collective-permute-start.118 = (f32[18,1,128]{2,1,0:T(1,128)S(1)}, f32[18,1,128]{2,1,0:T(1,128)S(1)}, u32[]{:S(2)}, u32[]{:S(2)}) collective-permute-start(f32[18,1,128]{2,1,0:T(1,128)S(1)} %get-tuple-element.55), channel_id=1, source_target_pairs={{0,1},{1,2},{2,3},{3,4},{4,5},{5,6},{6,7},{7,0},{8,9},{9,10},{10,1... | collective-permute-start | bytes 27656 | tf_op jit(solution)/shard_map/ppermute | solution.py:25
  693.5 9.5 %collective-permute-start.119 = (f32[18,1,128]{2,1,0:T(1,128)S(1)}, f32[18,1,128]{2,1,0:T(1,128)S(1)}, u32[]{:S(2)}, u32[]{:S(2)}) collective-permute-start(f32[18,1,128]{2,1,0:T(1,128)S(1)} %get-tuple-element.56), channel_id=1, source_target_pairs={{1,0},{2,1},{3,2},{4,3},{5,4},{6,5},{7,6},{0,7},{9,8},{10,9},{11,1... | collective-permute-start | bytes 27656 | tf_op jit(solution)/shard_map/ppermute | solution.py:27
  698.3 6.5 collective-permute-start.110
  (97 other events, 485.2 us)
where the time goes:
time: 758 us; the launch traced here: 759 us
  other arithmetic  379 us (50%)
  starting transfers between devices  195 us (26%)
  blocking collectives  77.4 us (10%)
  waiting for transfers between devices  71.9 us (9%)
  local copies, waits for them, and re-layouts  32.5 us (4%)
    scatter-add x1, other arithmetic, per_device(): jnp.zeros((block_cells + 1,), jnp.float32).at[target].add(masses)  360 us
    ppermute x60, starting transfers between devices, with_halo(): lax.ppermute(head, axis, [((i + 1) % count, i) for i in range(count)])  169 us
    ppermute x60, waiting for transfers between devices, with_halo(): lax.ppermute(tail, axis, [(i, (i + 1) % count) for i in range(count)])  67.8 us
    psum x1, blocking collectives, per_device(): square_sums.append(lax.psum(square_sum, ('gx', 'gy')))  40.4 us
    psum x1, blocking collectives, per_device(): lax.psum(jnp.sum(jnp.where(occupied, masses, 0.0)), ('gx', 'gy'))  37.1 us
    ppermute x60, starting transfers between devices, with_halo(): lax.ppermute(tail, axis, [(i, (i + 1) % count) for i in range(count)])  25.6 us
  transfers between devices with their start and end apart: 120, of which 50 were waited for; matrix products, arithmetic and copies ran while one was open for 51% of the time, Pallas kernels for 0%

commit v1 on v0

v1 whole, which is shorter than its diff:
```python
import functools

import jax
import jax.numpy as jnp
from jax import lax
from jax.experimental import pallas as pl
from jax.experimental.pallas import tpu as pltpu
from jax.sharding import PartitionSpec as P

CX = 16
CY = 8
NZ = 128
LEVELS = 4
CYCLES = 2
COARSE_SWEEPS = 2
HALO = 8

coupling = 0.03125
norm_eps = 1e-06

MESH = pl.DeviceIdType.MESH
F32 = jnp.float32
BF16 = jnp.bfloat16


def deposit_kernel(cell_ref, mass_ref, density_ref, sums_ref, acc_ref, msum_ref):
    rows = cell_ref.shape[0]
    step = 8
    cells = CX * CY
    acc_ref[...] = jnp.zeros_like(acc_ref)
    msum_ref[...] = jnp.zeros_like(msum_ref)

    def body(i, carry):
        at = pl.ds(pl.multiple_of(i * step, step), step)
        slot = cell_ref[at, :]
        mass = jnp.where(slot >= 0, mass_ref[at, :], 0.0)
        msum_ref[...] += mass
        high = mass.astype(BF16).astype(F32)
        rest = mass - high
        middle = rest.astype(BF16).astype(F32)
        low = rest - middle
        row = slot >> 7
        z = slot & (NZ - 1)
        row_ids = lax.broadcasted_iota(jnp.int32, (cells, 128), 0)
        z_ids = lax.broadcasted_iota(jnp.int32, (NZ, 128), 0)
        left, right = [], []
        for k in range(step):
            hit = row_ids == jnp.broadcast_to(row[k : k + 1], (cells, 128))
            pieces = [
                jnp.where(hit, jnp.broadcast_to(piece[k : k + 1], (cells, 128)), 0.0).astype(BF16)
                for piece in (high, middle, low)
            ]
            left.append(jnp.concatenate(pieces, axis=0))
            there = z_ids == jnp.broadcast_to(z[k : k + 1], (NZ, 128))
            right.append(jnp.where(there, 1.0, 0.0).astype(BF16))
        acc_ref[...] += lax.dot_general(
            jnp.concatenate(left, axis=1),
            jnp.concatenate(right, axis=1),
            (((1,), (1,)), ((), ())),
            preferred_element_type=F32,
        )
        return carry

    lax.fori_loop(0, rows // step, body, 0)
    density_ref[...] = acc_ref[0:cells] + (acc_ref[cells : 2 * cells] + acc_ref[2 * cells :])
    sums_ref[...] = jnp.sum(msum_ref[...], axis=0, keepdims=True)


def colour_of(shape, level):
    x = lax.broadcasted_iota(jnp.int32, shape, 0)
    y = lax.broadcasted_iota(jnp.int32, shape, 1)
    z = lax.broadcasted_iota(jnp.int32, shape, 2) >> level
    return (x + y + z) & 1


def chunk_of(planes, rows_y):
    chunk = 2
    while 2 * chunk * rows_y <= 128 and planes % (2 * chunk) == 0:
        chunk *= 2
    return chunk


def neighbours(u_ref, x0, chunk, level):
    planes, rows_y, lanes = u_ref.shape
    centre = u_ref[pl.ds(x0, chunk)]
    if chunk == planes:
        before, after = centre[planes - 1 :], centre[:1]
    else:
        before = u_ref[pl.ds(lax.rem(x0 + planes - 1, planes), 1)]
        after = u_ref[pl.ds(lax.rem(x0 + chunk, planes), 1)]
    total = jnp.concatenate([before, centre[:-1]], axis=0)
    total += jnp.concatenate([centre[1:], after], axis=0)
    total += pltpu.roll(centre, 1, 1) + pltpu.roll(centre, rows_y - 1, 1)
    stride = 2**level
    total += pltpu.roll(centre, stride, 2) + pltpu.roll(centre, lanes - stride, 2)
    return centre, total


def over_planes(planes, chunk, body, start=0):
    if planes == chunk:
        body(start)
        return

    def step(i, carry):
        body(start + i * chunk)
        return carry

    lax.fori_loop(0, planes // chunk, step, 0)


def relax(u_ref, b_ref, level, wanted):
    planes, rows_y, lanes = u_ref.shape
    chunk = chunk_of(planes, rows_y)
    spacing = float(4**level)

    def body(x0):
        centre, total = neighbours(u_ref, x0, chunk, level)
        new = (total + spacing * b_ref[pl.ds(x0, chunk)]) * (1.0 / 6.0)
        u_ref[pl.ds(x0, chunk)] = jnp.where(colour_of(centre.shape, level) == wanted, new, centre)

    over_planes(planes, chunk, body)


def sweep(u_ref, b_ref, level):
    relax(u_ref, b_ref, level, 0)
    relax(u_ref, b_ref, level, 1)


def first_sweep(u_ref, b_ref, level):
    planes, rows_y, lanes = u_ref.shape
    chunk = chunk_of(planes, rows_y)
    scale = float(4**level) / 6.0

    def body(x0):
        b = b_ref[pl.ds(x0, chunk)]
        u_ref[pl.ds(x0, chunk)] = jnp.where(colour_of(b.shape, level) == 0, b * scale, 0.0)

    over_planes(planes, chunk, body)
    relax(u_ref, b_ref, level, 1)


def pair_means(u_ref, b_ref, tmp_ref, level, x0, chunk):
    centre, total = neighbours(u_ref, x0, chunk, level)
    res = b_ref[pl.ds(x0, chunk)] - (6.0 * centre - total) * (1.0 / float(4**level))
    rows_y, lanes = res.shape[1:]
    pairs = res.reshape(chunk // 2, 2, rows_y, lanes)
    along_x = pairs[:, 0] + pairs[:, 1]
    stride = 2**level
    bit = (lax.broadcasted_iota(jnp.int32, along_x.shape, 2) >> level) & 1
    other = jnp.where(
        bit == 0, pltpu.roll(along_x, lanes - stride, 2), pltpu.roll(along_x, stride, 2)
    )
    tmp_ref[0 : chunk // 2, 0:rows_y, :] = (along_x + other) * 0.125


def y_pairs(tmp_ref, count, start, rows):
    return tmp_ref[0:count, pl.ds(start, rows, 2), :] + tmp_ref[0:count, pl.ds(start + 1, rows, 2), :]


def restrict(u_ref, b_ref, tmp_ref, coarse_ref, level):
    planes, rows_y, _ = u_ref.shape
    chunk = chunk_of(planes, rows_y)

    def body(x0):
        pair_means(u_ref, b_ref, tmp_ref, level, x0, chunk)
        coarse_ref[pl.ds(x0 // 2, chunk // 2)] = y_pairs(tmp_ref, chunk // 2, 0, rows_y // 2)

    over_planes(planes, chunk, body)


def spread_add(u_ref, coarse, tmp_ref, x0, chunk):
    half, rows, lanes = coarse.shape
    tmp_ref[0:half, pl.ds(0, rows, 2), :] = coarse
    tmp_ref[0:half, pl.ds(1, rows, 2), :] = coarse
    wide = tmp_ref[0:half, 0 : 2 * rows, :]
    wide = jnp.broadcast_to(wide[:, None], (half, 2, 2 * rows, lanes))
    u_ref[pl.ds(x0, chunk)] += wide.reshape(chunk, 2 * rows, lanes)


def prolong_add(u_ref, coarse_ref, tmp_ref):
    planes, rows_y, _ = u_ref.shape
    chunk = chunk_of(planes, rows_y)

    def body(x0):
        spread_add(u_ref, coarse_ref[pl.ds(x0 // 2, chunk // 2)], tmp_ref, x0, chunk)

    over_planes(planes, chunk, body)


def main_kernel(tiles_x, tiles_y, density_ref, sums_ref, potential_ref, residual_ref, norms_ref, *scratch):
    count = tiles_x * tiles_y
    (ext, b0, u0, mass_buf, norm_buf, norm_msg, packed, gathered, tmp) = scratch[:9]
    fields = scratch[9 : 9 + 2 * (LEVELS - 1)]
    halo_send, halo_recv, all_send, all_recv = scratch[9 + 2 * (LEVELS - 1) :]
    tile_x = lax.axis_index("gx")
    tile_y = lax.axis_index("gy")
    me = tile_x * tiles_y + tile_y
    grid_cells = CX * CY * NZ * count
    b = [b0] + [fields[2 * i] for i in range(LEVELS - 1)]
    u = [u0] + [fields[2 * i + 1] for i in range(LEVELS - 1)]

    def partner(k):
        d = lax.rem(me + k, count)
        return (d // tiles_y, lax.rem(d, tiles_y))

    barrier = pltpu.get_barrier_semaphore()

    def greet(k, carry):
        pl.semaphore_signal(barrier, inc=1, device_id=partner(k), device_id_type=MESH)
        return carry

    lax.fori_loop(1, count, greet, 0)
    pl.semaphore_wait(barrier, count - 1)

    def to_all(src, dst, which):
        def send(k, carry):
            pltpu.make_async_remote_copy(
                src_ref=src,
                dst_ref=dst.at[me],
                send_sem=all_send.at[which],
                recv_sem=all_recv.at[which],
                device_id=partner(k),
                device_id_type=MESH,
            ).start()
            return carry

        lax.fori_loop(1, count, send, 0)

    def from_all(dst, which):
        part = dst.at[pl.ds(0, count - 1)]
        pltpu.make_async_copy(part, part, all_recv.at[which]).wait()
        pltpu.make_async_copy(part, part, all_send.at[which]).wait()

    to_all(sums_ref, mass_buf, 0)
    halos = []
    for dx, dy in ((0, 1), (0, -1), (1, 1), (-1, 1), (1, -1), (-1, -1), (1, 0), (-1, 0)):
        rows = {1: (CX - HALO, HALO, 0), 0: (0, CX, HALO), -1: (0, HALO, HALO + CX)}[dx]
        to_y = {1: 0, 0: HALO, -1: HALO + CY}[dy]
        copy = pltpu.make_async_remote_copy(
            src_ref=density_ref.at[pl.ds(rows[0], rows[1])],
            dst_ref=ext.at[pl.ds(rows[2], rows[1]), pl.ds(to_y, CY), :],
            send_sem=halo_send.at[len(halos)],
            recv_sem=halo_recv.at[len(halos)],
            device_id=(
                lax.rem(tile_x + dx + tiles_x, tiles_x),
                lax.rem(tile_y + dy + tiles_y, tiles_y),
            ),
            device_id_type=MESH,
        )
        copy.start()
        halos.append(copy)
    ext[HALO : HALO + CX, HALO : HALO + CY, :] = density_ref[...]
    mass_buf[me] = sums_ref[...]
    from_all(mass_buf, 0)
    total_mass = jnp.sum(jnp.sum(mass_buf[...], axis=0), axis=-1, keepdims=True)
    scale = coupling / (total_mass / grid_cells)
    for copy in halos:
        copy.wait()

    planes0, rows0, _ = ext.shape
    chunk0 = 4

    def set_source(x0):
        at = pl.ds(x0, chunk0)
        b0[at] = coupling - ext[at] * jnp.broadcast_to(scale.reshape(1, 1, 1), (chunk0, rows0, NZ))

    over_planes(planes0, chunk0, set_source)

    lane = lax.broadcasted_iota(jnp.int32, (1, 1, NZ), 2) & 1
    half_x, half_y = CX // 2, CY // 2

    def coarse_correction(cycle_index):
        slot = packed.at[cycle_index]
        blocks = gathered.at[cycle_index]
        for part in range(CX // chunk0):
            pair_means(u0, b0, tmp, 0, HALO + part * chunk0, chunk0)
            b1_part = y_pairs(tmp, chunk0 // 2, HALO, half_y)
            for j in range(chunk0 // 2):
                plane = part * (chunk0 // 2) + j
                inner = plane % 4
                at = (inner % 2, slice(half_y * (inner // 2), half_y * (inner // 2 + 1)))
                if plane < 4:
                    packed[cycle_index, at[0], at[1], :] = b1_part[j]
                else:
                    old = packed[cycle_index, at[0], at[1], :]
                    packed[cycle_index, at[0], at[1], :] = jnp.where(lane[0] == 0, old, b1_part[j])
        to_all(slot, blocks, 1 + cycle_index)
        gathered[cycle_index, me] = packed[cycle_index]
        from_all(blocks, 1 + cycle_index)

        def unpack(i, carry):
            ix = i // (tiles_y // 2)
            iy = lax.rem(i, tiles_y // 2)
            first = gathered[cycle_index, ix * tiles_y + 2 * iy]
            second = gathered[cycle_index, ix * tiles_y + 2 * iy + 1]
            rows = pl.ds(pl.multiple_of(iy * 8, 8), 8)
            low = jnp.concatenate([first[:, :half_y], second[:, :half_y]], axis=1)
            high = jnp.concatenate([first[:, half_y:], second[:, half_y:]], axis=1)
            for offset, part in ((0, low), (2, high)):
                even = jnp.where(lane == 0, part, pltpu.roll(part, 1, 2))
                odd = jnp.where(lane == 1, part, pltpu.roll(part, NZ - 1, 2))
                b[1][pl.ds(ix * half_x + offset, 2), rows, :] = even
                b[1][pl.ds(ix * half_x + 4 + offset, 2), rows, :] = odd
            return carry

        lax.fori_loop(0, count // 2, unpack, 0)
        for level in range(1, LEVELS):
            first_sweep(u[level], b[level], level)
            if level < LEVELS - 1:
                restrict(u[level], b[level], tmp, b[level + 1], level)
        for _ in range(COARSE_SWEEPS - 1):
            sweep(u[LEVELS - 1], b[LEVELS - 1], LEVELS - 1)
        for level in range(LEVELS - 2, 0, -1):
            prolong_add(u[level], u[level + 1], tmp)
            sweep(u[level], b[level], level)

        rows1 = half_y * tiles_y
        planes1 = half_x * tiles_x
        start_y = half_y * tile_y - HALO // 2 + rows1
        tile = start_y // 8
        shifted = lax.rem(start_y, 8) != 0
        tile_a = pl.multiple_of(lax.rem(tile, rows1 // 8) * 8, 8)
        tile_b = pl.multiple_of(lax.rem(tile + 1, rows1 // 8) * 8, 8)
        start_x = half_x * tile_x - HALO // 2 + planes1

        def add(x0):
            parts = []
            for j in range(chunk0 // 2):
                plane = lax.rem(start_x + x0 // 2 + j, planes1)
                window = jnp.concatenate(
                    [u[1][plane, pl.ds(tile_a, 8), :], u[1][plane, pl.ds(tile_b, 8), :]], axis=0
                )
                width = half_y + HALO
                parts.append(jnp.where(shifted, window[4 : 4 + width], window[:width])[None])
            spread_add(u0, jnp.concatenate(parts, axis=0), tmp, x0, chunk0)

        over_planes(planes0, chunk0, add)

    def final_residual():
        sums = jnp.zeros((1, CY, NZ), F32)
        for part in range(CX // chunk0):
            x0 = HALO + part * chunk0
            centre, total = neighbours(u0, x0, chunk0, 0)
            res = (b0[pl.ds(x0, chunk0)] - (6.0 * centre - total)) * (1.0 / coupling)
            res = res[:, HALO : HALO + CY]
            residual_ref[pl.ds(part * chunk0, chunk0)] = res
            sums += jnp.sum(res * res, axis=0, keepdims=True)
        return jnp.sum(jnp.sum(sums[0], axis=0, keepdims=True), axis=1, keepdims=True)

    message = jnp.zeros((1, NZ), F32)
    lanes = lax.broadcasted_iota(jnp.int32, (1, NZ), 1)
    for cycle_index in range(CYCLES):
        if cycle_index == 0:
            first_sweep(u0, b0, 0)
        else:
            sweep(u0, b0, 0)
        coarse_correction(cycle_index)
        sweep(u0, b0, 0)
        message = jnp.where(lanes == cycle_index, final_residual(), message)
    norm_msg[...] = message
    potential_ref[...] = u0[HALO : HALO + CX, HALO : HALO + CY, :]
    to_all(norm_msg, norm_buf, 1 + CYCLES)
    norm_buf[me] = message
    from_all(norm_buf, 1 + CYCLES)
    totals = jnp.sum(norm_buf[...], axis=0)
    norms_ref[...] = jnp.sqrt(totals / grid_cells + norm_eps)


def per_device(tiles_x, tiles_y, particle_cell, particle_mass):
    slots = particle_cell.size
    vmem = pl.BlockSpec(memory_space=pltpu.VMEM)
    density, sums = pl.pallas_call(
        deposit_kernel,
        out_shape=(
            jax.ShapeDtypeStruct((CX * CY, NZ), F32),
            jax.ShapeDtypeStruct((1, 128), F32),
        ),
        in_specs=[vmem] * 2,
        out_specs=(vmem, vmem),
        scratch_shapes=[pltpu.VMEM((3 * CX * CY, NZ), F32), pltpu.VMEM((8, 128), F32)],
    )(particle_cell.reshape(slots // 128, 128), particle_mass.reshape(slots // 128, 128))

    count = tiles_x * tiles_y
    wide = (CX + 2 * HALO, CY + 2 * HALO, NZ)
    fields = []
    for level in range(1, LEVELS):
        shape = (CX * tiles_x >> level, CY * tiles_y >> level, NZ)
        fields += [pltpu.VMEM(shape, F32), pltpu.VMEM(shape, F32)]
    block = (CX, CY, NZ)
    tmp_rows = max(wide[1], CY * tiles_y // 2)
    potential, residual, norms = pl.pallas_call(
        functools.partial(main_kernel, tiles_x, tiles_y),
        out_shape=(
            jax.ShapeDtypeStruct(block, F32),
            jax.ShapeDtypeStruct(block, F32),
            jax.ShapeDtypeStruct((1, NZ), F32),
        ),
        in_specs=[vmem] * 2,
        out_specs=(vmem, vmem, vmem),
        scratch_shapes=[
            pltpu.VMEM(wide, F32),
            pltpu.VMEM(wide, F32),
            pltpu.VMEM(wide, F32),
            pltpu.VMEM((count, 1, NZ), F32),
            pltpu.VMEM((count, 1, NZ), F32),
            pltpu.VMEM((1, NZ), F32),
            pltpu.VMEM((CYCLES, 2, 8, NZ), F32),
            pltpu.VMEM((CYCLES, count, 2, 8, NZ), F32),
            pltpu.VMEM((16, tmp_rows, NZ), F32),
            *fields,
            pltpu.SemaphoreType.DMA((8,)),
            pltpu.SemaphoreType.DMA((8,)),
            pltpu.SemaphoreType.DMA((2 + CYCLES,)),
            pltpu.SemaphoreType.DMA((2 + CYCLES,)),
        ],
        compiler_params=pltpu.CompilerParams(collective_id=0, has_side_effects=True),
    )(density.reshape(block), sums)
    return potential, residual, norms[0, :CYCLES]


def solution(mesh):
    tiles_x, tiles_y = mesh.shape["gx"], mesh.shape["gy"]
    in_specs = (P("gx", "gy", None), P("gx", "gy", None))
    out_specs = (P("gx", "gy", None), P("gx", "gy", None), P())
    return jax.shard_map(
        functools.partial(per_device, tiles_x, tiles_y),
        mesh=mesh,
        in_specs=in_specs,
        out_specs=out_specs,
        check_vma=False,
    )
```

time: 758 us -> 88 us (0.12)
  other arithmetic: 379 us -> 0 us
  starting transfers between devices: 195 us -> 0 us
  Pallas kernels: 0 us -> 83.8 us
  blocking collectives: 77.4 us -> 0 us
  waiting for transfers between devices: 71.9 us -> 0 us
  local copies, waits for them, and re-layouts: 32.5 us -> 3.31 us
    scatter-add x1 -> x0, other arithmetic: 360 us -> none  [per_device(): jnp.zeros((block_cells + 1,), jnp.float32).at[target].add(masses)]
    ppermute x120 -> x0, starting transfers between devices: 195 us -> none  [the longest x60 169 us: with_halo(): lax.ppermute(head, axis, [((i + 1) % count, i) for i in range(count)])]
    pallas_call x0 -> x2, Pallas kernels: none -> 83.8 us  [the longest x1 57.8 us: per_device(): pl.pallas_call(functools.partial(main_kernel, tiles_x, tiles_y), out_shap...]
    psum x2 -> x0, blocking collectives: 77.4 us -> none  [the longest x1 40.4 us: per_device(): square_sums.append(lax.psum(square_sum, ('gx', 'gy')))]
    ppermute x120 -> x0, waiting for transfers between devices: 71.9 us -> none  [the longest x60 67.8 us: with_halo(): lax.ppermute(tail, axis, [(i, (i + 1) % count) for i in range(count)])]
    reshape x8 -> x0, local copies, waits for them, and re-layouts: 20.7 us -> none  [the longest x4 12.2 us: restrict(): values.reshape(rows_x // 2, 2, rows_y // 2, 2, rows_z // 2, 2)]
    reduce_sum x11 -> x0, other arithmetic: 9.45 us -> none  [the longest x8 5.71 us: restrict(): values.reshape(rows_x // 2, 2, rows_y // 2, 2, rows_z // 2, 2)]
  transfers between devices with their start and end apart: 120 -> 0, of which waited for: 50 -> 0; matrix products, arithmetic and copies ran while one was open for 51% -> 0% of each run, Pallas kernels for 0% -> 0%
where the time goes in v1:
time: 88 us; the launch traced here: 87.7 us
  Pallas kernels  83.8 us (95%)
  local copies, waits for them, and re-layouts  3.31 us (4%)
    pallas_call x1, Pallas kernels, per_device(): pl.pallas_call(functools.partial(main_kernel, tiles_x, tiles_y), out_shap...  57.8 us
    pallas_call x1, Pallas kernels, per_device(): pl.pallas_call(deposit_kernel, out_shape=(jax.ShapeDtypeStruct((CX * CY,...  25.9 us
    unnamed x6, local copies, waits for them, and re-layouts  2.8 us

profile of v1, /device:TPU:0, one launch (start us, length us, event | category | flops | bytes accessed | tf_op | source)
XLA Modules:
  0.0 87.7 jit_solution(17321799008592363881)
XLA Ops:
  0.6 25.9 %shard_map.49 = (f32[128,128]{1,0:T(8,128)}, f32[1,128]{1,0:T(1,128)}) custom-call(s32[512,128]{1,0:T(8,128)} %bitcast.5, f32[512,128]{1,0:T(8,128)} %bitcast.6), custom_call_target="tpu_custom_call" | custom-call | tf_op jit(solution)/shard_map/pallas_call | solution.py:372
  26.6 57.8 %shard_map.50 = (f32[16,8,128]{2,1,0:T(8,128)}, f32[16,8,128]{2,1,0:T(8,128)}, f32[1,128]{1,0:T(1,128)}) custom-call(f32[16,8,128]{2,1,0:T(8,128)} %bitcast.7, f32[1,128]{1,0:T(1,128)} %get-tuple-element.9.sums_ref), custom_call_target="tpu_custom_call" | custom-call | tf_op jit(solution)/shard_map/pallas_call | solution.py:391
  84.4 0.0 copy-start.1
  84.4 0.7 copy-done.1
  85.1 0.5 slice_bitcast_fusion
  85.6 0.0 copy-start
  85.6 1.5 %copy.7 = f32[16,8,128]{2,1,0:T(8,128)} copy(f32[16,8,128]{2,1,0:T(8,128)} %get-tuple-element.16) | data formatting | bytes 131072
  87.1 0.0 copy-done
  87.1 0.6 copy.8
Async XLA Ops:
  84.4 0.7 copy-start.1
  85.6 1.5 %copy-start = (f32[16,8,128]{2,1,0:T(8,128)S(1)}, f32[16,8,128]{2,1,0:T(8,128)}, u32[]{:S(2)}) copy-start(f32[16,8,128]{2,1,0:T(8,128)} %get-tuple-element.17) | copy-start | bytes 196612

commit v2 on v1

--- a/solution.py
+++ b/solution.py
@@ -26,7 +26,8 @@
 def deposit_kernel(cell_ref, mass_ref, density_ref, sums_ref, acc_ref, msum_ref):
     rows = cell_ref.shape[0]
     step = 8
-    cells = CX * CY
+    cells = CX * CY // 2
+    wide = 2 * NZ
     acc_ref[...] = jnp.zeros_like(acc_ref)
     msum_ref[...] = jnp.zeros_like(msum_ref)
 
@@ -39,20 +40,27 @@
         rest = mass - high
         middle = rest.astype(BF16).astype(F32)
         low = rest - middle
-        row = slot >> 7
-        z = slot & (NZ - 1)
-        row_ids = lax.broadcasted_iota(jnp.int32, (cells, 128), 0)
-        z_ids = lax.broadcasted_iota(jnp.int32, (NZ, 128), 0)
+        row = (slot >> 8).astype(F32)
+        z = (slot & (wide - 1)).astype(F32)
+
+        def pair(values, k):
+            return jnp.broadcast_to(values[k : k + 1], (16, 128)).astype(BF16)
+
+        ids = lax.broadcasted_iota(jnp.int32, (16, 128), 0)
+        ids = [(ids + 16 * j).astype(F32).astype(BF16) for j in range(max(cells, wide) // 16)]
+        one, zero = jnp.ones((16, 128), BF16), jnp.zeros((16, 128), BF16)
         left, right = [], []
         for k in range(step):
-            hit = row_ids == jnp.broadcast_to(row[k : k + 1], (cells, 128))
-            pieces = [
-                jnp.where(hit, jnp.broadcast_to(piece[k : k + 1], (cells, 128)), 0.0).astype(BF16)
-                for piece in (high, middle, low)
-            ]
+            at_row, at_z = pair(row, k), pair(z, k)
+            hits = [at_row == ids[j] for j in range(cells // 16)]
+            pieces = []
+            for values in (high, middle, low):
+                piece = pair(values, k)
+                pieces += [jnp.where(hit, piece, zero) for hit in hits]
             left.append(jnp.concatenate(pieces, axis=0))
-            there = z_ids == jnp.broadcast_to(z[k : k + 1], (NZ, 128))
-            right.append(jnp.where(there, 1.0, 0.0).astype(BF16))
+            right.append(
+                jnp.concatenate([jnp.where(at_z == ids[j], one, zero) for j in range(wide // 16)], axis=0)
+            )
         acc_ref[...] += lax.dot_general(
             jnp.concatenate(left, axis=1),
             jnp.concatenate(right, axis=1),
@@ -62,7 +70,9 @@
         return carry
 
     lax.fori_loop(0, rows // step, body, 0)
-    density_ref[...] = acc_ref[0:cells] + (acc_ref[cells : 2 * cells] + acc_ref[2 * cells :])
+    density = acc_ref[0:cells] + (acc_ref[cells : 2 * cells] + acc_ref[2 * cells :])
+    density_ref[pl.ds(0, cells, 2), :] = density[:, :NZ]
+    density_ref[pl.ds(1, cells, 2), :] = density[:, NZ:]
     sums_ref[...] = jnp.sum(msum_ref[...], axis=0, keepdims=True)
 
 
@@ -78,6 +88,10 @@
     while 2 * chunk * rows_y <= 128 and planes % (2 * chunk) == 0:
         chunk *= 2
     return chunk
+
+
+def wrapped(x, planes):
+    return x % planes if isinstance(x, int) else lax.rem(x, planes)
 
 
 def neighbours(u_ref, x0, chunk, level):
@@ -86,8 +100,8 @@
     if chunk == planes:
         before, after = centre[planes - 1 :], centre[:1]
     else:
-        before = u_ref[pl.ds(lax.rem(x0 + planes - 1, planes), 1)]
-        after = u_ref[pl.ds(lax.rem(x0 + chunk, planes), 1)]
+        before = u_ref[pl.ds(wrapped(x0 + planes - 1, planes), 1)]
+        after = u_ref[pl.ds(wrapped(x0 + chunk, planes), 1)]
     total = jnp.concatenate([before, centre[:-1]], axis=0)
     total += jnp.concatenate([centre[1:], after], axis=0)
     total += pltpu.roll(centre, 1, 1) + pltpu.roll(centre, rows_y - 1, 1)
@@ -97,8 +111,9 @@
 
 
 def over_planes(planes, chunk, body, start=0):
-    if planes == chunk:
-        body(start)
+    if planes // chunk <= 8:
+        for i in range(planes // chunk):
+            body(start + i * chunk)
         return
 
     def step(i, carry):
@@ -191,10 +206,13 @@
     count = tiles_x * tiles_y
     (ext, b0, u0, mass_buf, norm_buf, norm_msg, packed, gathered, tmp) = scratch[:9]
     fields = scratch[9 : 9 + 2 * (LEVELS - 1)]
-    halo_send, halo_recv, all_send, all_recv = scratch[9 + 2 * (LEVELS - 1) :]
+    halo_send, halo_recv, all_send, all_recv, pass_send, pass_recv = scratch[9 + 2 * (LEVELS - 1) :]
     tile_x = lax.axis_index("gx")
     tile_y = lax.axis_index("gy")
     me = tile_x * tiles_y + tile_y
+    side = lax.rem(tile_x, 2)
+    pairs = count // 2
+    my_pair = (tile_x // 2) * tiles_y + tile_y
     grid_cells = CX * CY * NZ * count
     b = [b0] + [fields[2 * i] for i in range(LEVELS - 1)]
     u = [u0] + [fields[2 * i + 1] for i in range(LEVELS - 1)]
@@ -270,8 +288,6 @@
     half_x, half_y = CX // 2, CY // 2
 
     def coarse_correction(cycle_index):
-        slot = packed.at[cycle_index]
-        blocks = gathered.at[cycle_index]
         for part in range(CX // chunk0):
             pair_means(u0, b0, tmp, 0, HALO + part * chunk0, chunk0)
             b1_part = y_pairs(tmp, chunk0 // 2, HALO, half_y)
@@ -284,16 +300,41 @@
                 else:
                     old = packed[cycle_index, at[0], at[1], :]
                     packed[cycle_index, at[0], at[1], :] = jnp.where(lane[0] == 0, old, b1_part[j])
-        to_all(slot, blocks, 1 + cycle_index)
-        gathered[cycle_index, me] = packed[cycle_index]
-        from_all(blocks, 1 + cycle_index)
-
-        def unpack(i, carry):
-            ix = i // (tiles_y // 2)
-            iy = lax.rem(i, tiles_y // 2)
-            first = gathered[cycle_index, ix * tiles_y + 2 * iy]
-            second = gathered[cycle_index, ix * tiles_y + 2 * iy + 1]
-            rows = pl.ds(pl.multiple_of(iy * 8, 8), 8)
+        which = 1 + cycle_index
+
+        def send(k, carry):
+            pair = lax.rem(my_pair + k, pairs)
+            pltpu.make_async_remote_copy(
+                src_ref=packed.at[cycle_index],
+                dst_ref=gathered.at[cycle_index, side, my_pair],
+                send_sem=all_send.at[which],
+                recv_sem=all_recv.at[which],
+                device_id=(2 * (pair // tiles_y) + side, lax.rem(pair, tiles_y)),
+                device_id_type=MESH,
+            ).start()
+            return carry
+
+        lax.fori_loop(1, pairs, send, 0)
+        gathered[cycle_index, side, my_pair] = packed[cycle_index]
+        arrived = gathered.at[cycle_index, 0, pl.ds(0, pairs - 1)]
+        pltpu.make_async_copy(arrived, arrived, all_recv.at[which]).wait()
+        pltpu.make_async_copy(arrived, arrived, all_send.at[which]).wait()
+        forward = pltpu.make_async_remote_copy(
+            src_ref=gathered.at[cycle_index, side],
+            dst_ref=gathered.at[cycle_index, side],
+            send_sem=pass_send.at[cycle_index],
+            recv_sem=pass_recv.at[cycle_index],
+            device_id=(tile_x + 1 - 2 * side, tile_y),
+            device_id_type=MESH,
+        )
+        forward.start()
+        forward.wait()
+
+        def unpack(ix, side_x, iy):
+            pair = (ix // 2) * tiles_y + 2 * iy
+            first = gathered[cycle_index, side_x, pair]
+            second = gathered[cycle_index, side_x, pair + 1]
+            rows = slice(iy * 8, iy * 8 + 8)
             low = jnp.concatenate([first[:, :half_y], second[:, :half_y]], axis=1)
             high = jnp.concatenate([first[:, half_y:], second[:, half_y:]], axis=1)
             for offset, part in ((0, low), (2, high)):
@@ -301,9 +342,13 @@
                 odd = jnp.where(lane == 1, part, pltpu.roll(part, NZ - 1, 2))
                 b[1][pl.ds(ix * half_x + offset, 2), rows, :] = even
                 b[1][pl.ds(ix * half_x + 4 + offset, 2), rows, :] = odd
-            return carry
-
-        lax.fori_loop(0, count // 2, unpack, 0)
+
+        def unpack_rows(x0):
+            for side_x in range(2):
+                for iy in range(tiles_y // 2):
+                    unpack(x0 + side_x, side_x, iy)
+
+        over_planes(tiles_x, 2, unpack_rows)
         for level in range(1, LEVELS):
             first_sweep(u[level], b[level], level)
             if level < LEVELS - 1:
@@ -377,7 +422,7 @@
         ),
         in_specs=[vmem] * 2,
         out_specs=(vmem, vmem),
-        scratch_shapes=[pltpu.VMEM((3 * CX * CY, NZ), F32), pltpu.VMEM((8, 128), F32)],
+        scratch_shapes=[pltpu.VMEM((3 * CX * CY // 2, 2 * NZ), F32), pltpu.VMEM((8, 128), F32)],
     )(particle_cell.reshape(slots // 128, 128), particle_mass.reshape(slots // 128, 128))
 
     count = tiles_x * tiles_y
@@ -405,13 +450,15 @@
             pltpu.VMEM((count, 1, NZ), F32),
             pltpu.VMEM((1, NZ), F32),
             pltpu.VMEM((CYCLES, 2, 8, NZ), F32),
-            pltpu.VMEM((CYCLES, count, 2, 8, NZ), F32),
+            pltpu.VMEM((CYCLES, 2, count // 2, 2, 8, NZ), F32),
             pltpu.VMEM((16, tmp_rows, NZ), F32),
             *fields,
             pltpu.SemaphoreType.DMA((8,)),
             pltpu.SemaphoreType.DMA((8,)),
             pltpu.SemaphoreType.DMA((2 + CYCLES,)),
             pltpu.SemaphoreType.DMA((2 + CYCLES,)),
+            pltpu.SemaphoreType.DMA((CYCLES,)),
+            pltpu.SemaphoreType.DMA((CYCLES,)),
         ],
         compiler_params=pltpu.CompilerParams(collective_id=0, has_side_effects=True),
     )(density.reshape(block), sums)

time: 88 us -> 69.7 us (0.79)
  Pallas kernels: 83.8 us -> 65.5 us
    pallas_call x1, Pallas kernels: 57.8 us -> 42.1 us  [per_device(): pl.pallas_call(functools.partial(main_kernel, tiles_x, tiles_y), out_shap...]
    pallas_call x1, Pallas kernels: 25.9 us -> 23.4 us  [per_device(): pl.pallas_call(deposit_kernel, out_shape=(jax.ShapeDtypeStruct((CX * CY,...]
where the time goes in v2:
time: 69.7 us; the launch traced here: 69.5 us
  Pallas kernels  65.5 us (94%)
  local copies, waits for them, and re-layouts  3.31 us (5%)
    pallas_call x1, Pallas kernels, per_device(): pl.pallas_call(functools.partial(main_kernel, tiles_x, tiles_y), out_shap...  42.1 us
    pallas_call x1, Pallas kernels, per_device(): pl.pallas_call(deposit_kernel, out_shape=(jax.ShapeDtypeStruct((CX * CY,...  23.4 us
    unnamed x6, local copies, waits for them, and re-layouts  2.8 us

profile of v2, /device:TPU:0, one launch (start us, length us, event | category | flops | bytes accessed | tf_op | source)
XLA Modules:
  0.0 69.5 jit_solution(7245498099049715360)
XLA Ops:
  0.6 23.4 %shard_map.49 = (f32[128,128]{1,0:T(8,128)}, f32[1,128]{1,0:T(1,128)}) custom-call(s32[512,128]{1,0:T(8,128)} %bitcast.5, f32[512,128]{1,0:T(8,128)} %bitcast.6), custom_call_target="tpu_custom_call" | custom-call | tf_op jit(solution)/shard_map/pallas_call | solution.py:417
  24.0 42.1 %shard_map.50 = (f32[16,8,128]{2,1,0:T(8,128)}, f32[16,8,128]{2,1,0:T(8,128)}, f32[1,128]{1,0:T(1,128)}) custom-call(f32[16,8,128]{2,1,0:T(8,128)} %bitcast.7, f32[1,128]{1,0:T(1,128)} %get-tuple-element.9.sums_ref), custom_call_target="tpu_custom_call" | custom-call | tf_op jit(solution)/shard_map/pallas_call | solution.py:436
  66.2 0.0 copy-start.1
  66.2 0.7 copy-done.1
  66.8 0.5 slice_bitcast_fusion
  67.3 0.0 copy-start
  67.3 1.5 %copy.7 = f32[16,8,128]{2,1,0:T(8,128)} copy(f32[16,8,128]{2,1,0:T(8,128)} %get-tuple-element.16) | data formatting | bytes 131072
  68.8 0.0 copy-done
  68.8 0.6 copy.8
Async XLA Ops:
  66.2 0.7 copy-start.1
  67.3 1.5 %copy-start = (f32[16,8,128]{2,1,0:T(8,128)S(1)}, f32[16,8,128]{2,1,0:T(8,128)}, u32[]{:S(2)}) copy-start(f32[16,8,128]{2,1,0:T(8,128)} %get-tuple-element.17) | copy-start | bytes 196612
